TPU v7x, 32 devices: a whole 2x2x4 slice. The times are simulated.
32 devices in a mesh: dp: 8 (over y, x, core), mp: 4 (over z).
Axes of the slice: x: 2, y: 2, z: 4, core: 2. Of those that a mesh axis runs over, the one named last changes fastest.
Arguments:
- layer_input: bfloat16 [32, 8192], P('dp'), may hold values from -6 to 6
- pre_act: bfloat16 [32, 8192], P('dp', 'mp'), may hold values from -8 to 8
- hidden_adjoint: bfloat16 [32, 8192], P('dp', 'mp'), may hold values from -6 to 6
- output_adjoint: bfloat16 [32, 8192], P('dp', 'mp'), may hold values from -6 to 6
Outputs:
- precond_in: float32 [8192, 8192], P('dp', 'mp')
- direction_in: float32 [8192, 8192], P('dp', 'mp')
- precond_out: float32 [8192, 8192], P('dp', 'mp')
- direction_out: float32 [8192, 8192], P('dp', 'mp')
- sq_norm: float32 [], replicated
All inputs are finite; a program needn't handle non-finite values.
Results may differ from a plain program's by a relative error of at most 0.0029.
Values may be sent and summed in bfloat16 or wider, within the bound.
A program may use at most 64 MiB of HBM per device.

v0:
```python
import jax
import jax.numpy as jnp
from jax import lax
from jax.sharding import PartitionSpec as P

D = 8192
H = 8192
DAMPING = 0.1
EXPONENT = 0.75


def square_bf(values):
    wide = values.astype(jnp.float32)
    return (wide * wide).astype(jnp.bfloat16)


def accumulate(act_block, sq_block, adj_piece):
    contract = (((0,), (0,)), ((), ()))
    grad_sum = lax.dot_general(act_block, adj_piece, contract, preferred_element_type=jnp.float32)
    square_sum = lax.dot_general(
        sq_block, square_bf(adj_piece), contract, preferred_element_type=jnp.float32
    )
    return (grad_sum, square_sum)


def finish(partial_value, total_rows):
    gradient = partial_value[0] / total_rows
    precond = (partial_value[1] / total_rows + DAMPING) ** EXPONENT
    norm_term = jnp.sum(gradient * gradient / precond)
    return (gradient, precond, norm_term)


def shards(layer_input, pre_act, hidden_adjoint, output_adjoint):
    preact = pre_act.astype(jnp.float32)
    logistic = jax.nn.sigmoid(preact)
    hidden = (preact * logistic).astype(jnp.bfloat16)
    adjoint = (
        hidden_adjoint.astype(jnp.float32) * logistic * (1.0 + preact * (1.0 - logistic))
    ).astype(jnp.bfloat16)
    own_input = lax.all_to_all(layer_input, "dp", split_axis=1, concat_axis=0, tiled=True)
    sq_input = square_bf(own_input)
    total_rows = own_input.shape[0]
    wide_hidden = lax.all_gather(hidden, "mp", axis=1, tiled=True)
    own_hidden = lax.all_to_all(wide_hidden, "dp", split_axis=1, concat_axis=0, tiled=True)
    sq_hidden = square_bf(own_hidden)
    sums_in = accumulate(own_input, sq_input, lax.all_gather(adjoint, "dp", axis=0, tiled=True))
    sums_out = accumulate(
        own_hidden, sq_hidden, lax.all_gather(output_adjoint, "dp", axis=0, tiled=True)
    )
    gradient_in, precond_in, term_in = finish(sums_in, total_rows)
    gradient_out, precond_out, term_out = finish(sums_out, total_rows)
    sq_norm = lax.psum(term_in + term_out, ("dp", "mp"))
    rescale = jnp.sqrt(2.0 * D * H / sq_norm)
    direction_in = gradient_in / precond_in * rescale
    direction_out = gradient_out / precond_out * rescale
    return (precond_in, direction_in, precond_out, direction_out, sq_norm)


def solution(mesh):
    placed = (P("dp", None), P("dp", "mp"), P("dp", "mp"), P("dp", "mp"))
    return jax.shard_map(
        shards,
        mesh=mesh,
        in_specs=placed,
        out_specs=(P("dp", "mp"), P("dp", "mp"), P("dp", "mp"), P("dp", "mp"), P()),
        check_vma=False,
    )
```

profile of v0, /device:TPU:0, one launch (start us, length us, event | category | flops | bytes accessed | tf_op | source)
XLA Modules:
  0.0 133.4 jit_solution(15350232104087235126)
XLA Ops:
  0.6 5.2 %all-to-all-start = ((bf16[4,8,1024]{2,0,1:T(4,128)(2,1)}), bf16[4,8,1024]{2,0,1:T(4,128)(2,1)S(1)}, u32[]{:S(2)}, u32[]{:S(2)}) async-start(bf16[4,8,1024]{2,0,1:T(4,128)(2,1)} %bitcast.22), calls=%async_computation | async-start | bytes 131072 | tf_op jit(solution)/shard_map/all_to_all | solution.py:40
  5.8 0.8 fusion.13
  6.6 14.1 %all_gather.10 = bf16[4,8192]{1,0:T(4,128)(2,1)} all-gather(bf16[4,2048]{1,0:T(4,128)(2,1)S(1)} %get-tuple-element.9), channel_id=1, replica_groups=mesh['dp'=8,'mp'=4] {'mp'}, dimensions={1}, use_global_device_ids=true | all-gather | bytes 81920 | tf_op jit(solution)/shard_map/all_gather | solution.py:43
  20.7 0.0 all-to-all-done
  20.7 4.3 %all-to-all-start.1 = ((bf16[4,8,1024]{2,0,1:T(4,128)(2,1)}), bf16[4,8,1024]{2,0,1:T(4,128)(2,1)S(1)}, u32[]{:S(2)}, u32[]{:S(2)}) async-start(bf16[4,8,1024]{2,0,1:T(4,128)(2,1)} %bitcast.4), calls=%async_computation.1 | async-start | bytes 131072 | tf_op jit(solution)/shard_map/all_to_all | solution.py:44
  25.0 9.7 %all-gather = bf16[8,4,2048]{2,1,0:T(4,128)(2,1)S(1)} all-gather(bf16[1,4,2048]{2,1,0:T(4,128)(2,1)S(1)} %get-tuple-element.10), channel_id=1, replica_groups=mesh['dp'=8,'mp'=4] {'dp'}, dimensions={0}, use_global_device_ids=true | all-gather | bytes 147456 | tf_op jit(solution)/shard_map/all_gather | solution.py:46
  34.7 9.2 %all-gather.1 = bf16[8,4,2048]{2,1,0:T(4,128)(2,1)S(1)} all-gather(bf16[1,4,2048]{2,1,0:T(4,128)(2,1)} %bitcast.23), channel_id=1, replica_groups=mesh['dp'=8,'mp'=4] {'dp'}, dimensions={0}, use_global_device_ids=true | all-gather | bytes 147456 | tf_op jit(solution)/shard_map/all_gather | solution.py:48
  44.0 0.0 all-to-all-done.1
  44.0 1.3 fusion.6
  45.3 0.0 copy-start
  45.3 7.8 %multiply_reduce_fusion = (f32[]{:T(128)}, f32[1024,2048]{1,0:T(8,128)}) fusion(f32[1024,2048]{1,0:T(8,128)S(1)} %fusion.6, bf16[32,1024]{1,0:T(8,128)(2,1)S(1)} %all_to_all.35, bf16[32,2048]{1,0:T(8,128)(2,1)S(1)} %reshape.19), kind=kOutput, calls=%fused_computation.6 | convolution fusion | flops 146800640 | bytes 16973828 | tf_op jit(solution)/shard_map/dot_general | solution.py:19
  53.1 0.0 copy-done
  53.1 1.3 fusion.5
  54.3 0.0 copy-start.1
  54.4 7.7 %fusion.2 = (f32[]{:T(128)}, f32[2048,1024]{0,1:T(8,128)}) fusion(f32[1024,2048]{1,0:T(8,128)S(1)} %fusion.5, bf16[32,2048]{1,0:T(8,128)(2,1)S(1)} %reshape.17, bf16[32,1024]{1,0:T(8,128)(2,1)S(1)} %all_to_all.31), kind=kOutput, calls=%fused_computation.4 | convolution fusion | flops 146800640 | bytes 16973828 | tf_op jit(solution)/shard_map/dot_general | solution.py:19
  62.0 0.0 copy-done.1
  63.3 39.4 %psum.7 = f32[]{:T(128)} all-reduce(f32[]{:T(128)S(6)} %add.21), channel_id=1, replica_groups=mesh['dp'=8,'mp'=4] {'dp','mp'}, use_global_device_ids=true, to_apply=%region_2.0 | all-reduce | flops 1 | bytes 8 | tf_op jit(solution)/shard_map/psum | solution.py:52
  103.5 29.9 %fusion = (f32[1024,2048]{1,0:T(8,128)}, f32[1024,2048]{1,0:T(8,128)}, f32[1024,2048]{1,0:T(8,128)}, f32[1024,2048]{1,0:T(8,128)}) fusion(f32[2048,1024]{0,1:T(8,128)} %get-tuple-element.12, f32[1024,2048]{1,0:T(8,128)} %copy-done.1, f32[]{:T(128)S(6)} %sqrt.3, f32[1024,2048]{1,0:T(8,128)} %copy-done, f32[1024,2048]{1,0:T(8,128)} %get-tuple-element.14), kind=kLoop, calls=%fused_computation.2 | loop fusion | flops 20971520 | bytes 67108864 | tf_op jit(solution)/shard_map/mul | solution.py:54
  (4 shorter events, 0.1 us)
Async XLA Ops:
  0.6 20.1 %all-to-all-start = ((bf16[4,8,1024]{2,0,1:T(4,128)(2,1)}), bf16[4,8,1024]{2,0,1:T(4,128)(2,1)S(1)}, u32[]{:S(2)}, u32[]{:S(2)}) async-start(bf16[4,8,1024]{2,0,1:T(4,128)(2,1)} %bitcast.22), calls=%async_computation | async-start | bytes 131072 | tf_op jit(solution)/shard_map/all_to_all | solution.py:40
  20.7 23.2 %all-to-all-start.1 = ((bf16[4,8,1024]{2,0,1:T(4,128)(2,1)}), bf16[4,8,1024]{2,0,1:T(4,128)(2,1)S(1)}, u32[]{:S(2)}, u32[]{:S(2)}) async-start(bf16[4,8,1024]{2,0,1:T(4,128)(2,1)} %bitcast.4), calls=%async_computation.1 | async-start | bytes 131072 | tf_op jit(solution)/shard_map/all_to_all | solution.py:44
  45.3 7.8 %copy-start = (f32[1024,2048]{1,0:T(8,128)}, f32[1024,2048]{1,0:T(8,128)S(1)}, u32[]{:S(2)}) copy-start(f32[1024,2048]{1,0:T(8,128)S(1)} %fusion.6) | copy-start | bytes 25165828
  54.3 7.7 %copy-start.1 = (f32[1024,2048]{1,0:T(8,128)}, f32[1024,2048]{1,0:T(8,128)S(1)}, u32[]{:S(2)}) copy-start(f32[1024,2048]{1,0:T(8,128)S(1)} %fusion.5) | copy-start | bytes 25165828
where the time goes:
time: 134 us; the launch traced here: 133 us
  blocking collectives  72.4 us (54%)
  other arithmetic  30.6 us (23%)
  matrix products  18 us (13%)
  starting transfers between devices  9.48 us (7%)
  between operations  2.7 us (2%)
    psum x1, blocking collectives, shards(): sq_norm = lax.psum(term_in + term_out, ('dp', 'mp'))  39.4 us
    mul x1, other arithmetic, shards(): direction_in = gradient_in / precond_in * rescale  29.9 us
    dot_general x2, matrix products, accumulate(): lax.dot_general(act_block, adj_piece, contract, preferred_element_type=jn...  15.4 us
    all_gather x1, blocking collectives, shards(): wide_hidden = lax.all_gather(hidden, 'mp', axis=1, tiled=True)  14.1 us
    all_gather x1, blocking collectives, shards(): lax.all_gather(adjoint, 'dp', axis=0, tiled=True)  9.71 us
    all_gather x1, blocking collectives, shards(): lax.all_gather(output_adjoint, 'dp', axis=0, tiled=True)  9.16 us
    all_to_all x1, starting transfers between devices, shards(): lax.all_to_all(layer_input, 'dp', split_axis=1, concat_axis=0, tiled=True)  5.21 us
    all_to_all x1, starting transfers between devices, shards(): lax.all_to_all(wide_hidden, 'dp', split_axis=1, concat_axis=0, tiled=True)  4.27 us
  transfers between devices with their start and end apart: 2, of which 0 were waited for; matrix products, arithmetic and copies ran while one was open for 1% of the time, Pallas kernels for 0%

commit v1 on v0

--- a/solution.py
+++ b/solution.py
@@ -40,7 +40,12 @@
     own_input = lax.all_to_all(layer_input, "dp", split_axis=1, concat_axis=0, tiled=True)
     sq_input = square_bf(own_input)
     total_rows = own_input.shape[0]
-    wide_hidden = lax.all_gather(hidden, "mp", axis=1, tiled=True)
+    ring = [hidden]
+    for hop in range(3):
+        ring.append(lax.ppermute(ring[-1], "mp", [(dev, (dev + 1) % 4) for dev in range(4)]))
+    wide_hidden = jnp.roll(
+        jnp.concatenate(ring[::-1], axis=1), (lax.axis_index("mp") + 1) * ring[0].shape[1], axis=1
+    )
     own_hidden = lax.all_to_all(wide_hidden, "dp", split_axis=1, concat_axis=0, tiled=True)
     sq_hidden = square_bf(own_hidden)
     sums_in = accumulate(own_input, sq_input, lax.all_gather(adjoint, "dp", axis=0, tiled=True))

time: 134 us -> 130 us (0.970)
  blocking collectives: 72.4 us -> 58.5 us
  local copies, waits for them, and re-layouts: 0.12 us -> 4.25 us
  starting transfers between devices: 9.48 us -> 13.4 us
  other arithmetic: 30.6 us -> 32.2 us
    all_gather x1 -> x0, blocking collectives: 14.1 us -> none  [shards(): wide_hidden = lax.all_gather(hidden, 'mp', axis=1, tiled=True)]
    ppermute x0 -> x3, starting transfers between devices: none -> 6.35 us  [shards(): lax.ppermute(ring[-1], 'mp', [(dev, (dev + 1) % 4) for dev in range(4)])]
    unnamed x6 -> x12, local copies, waits for them, and re-layouts: 0.08 us -> 3.55 us
    all_to_all x1, starting transfers between devices: 5.21 us -> 3.72 us  [shards(): lax.all_to_all(layer_input, 'dp', split_axis=1, concat_axis=0, tiled=True)]
  transfers between devices with their start and end apart: 2 -> 5, of which waited for: 0 -> 0; matrix products, arithmetic and copies ran while one was open for 1% -> 9% of each run, Pallas kernels for 0% -> 0%
where the time goes in v1:
time: 130 us; the launch traced here: 129 us
  blocking collectives  58.5 us (45%)
  other arithmetic  32.2 us (25%)
  matrix products  18 us (14%)
  starting transfers between devices  13.4 us (10%)
  local copies, waits for them, and re-layouts  4.25 us (3%)
  between operations  2.74 us (2%)
    psum x1, blocking collectives, shards(): sq_norm = lax.psum(term_in + term_out, ('dp', 'mp'))  39.7 us
    mul x1, other arithmetic, shards(): direction_in = gradient_in / precond_in * rescale  29.9 us
    dot_general x2, matrix products, accumulate(): lax.dot_general(act_block, adj_piece, contract, preferred_element_type=jn...  15.4 us
    all_gather x1, blocking collectives, shards(): lax.all_gather(adjoint, 'dp', axis=0, tiled=True)  9.65 us
    all_gather x1, blocking collectives, shards(): lax.all_gather(output_adjoint, 'dp', axis=0, tiled=True)  9.14 us
    ppermute x3, starting transfers between devices, shards(): lax.ppermute(ring[-1], 'mp', [(dev, (dev + 1) % 4) for dev in range(4)])  6.35 us
    all_to_all x1, starting transfers between devices, shards(): lax.all_to_all(layer_input, 'dp', split_axis=1, concat_axis=0, tiled=True)  3.72 us
    unnamed x12, local copies, waits for them, and re-layouts  3.55 us
  transfers between devices with their start and end apart: 5, of which 0 were waited for; matrix products, arithmetic and copies ran while one was open for 9% of the time, Pallas kernels for 0%

profile of v1, /device:TPU:0, one launch (start us, length us, event | category | flops | bytes accessed | tf_op | source)
XLA Modules:
  0.0 129.1 jit_solution(1162542685582596170)
XLA Ops:
  0.6 0.8 fusion.13
  1.4 3.1 %collective-permute-start = (bf16[4,2048]{1,0:T(4,128)(2,1)S(1)}, bf16[4,2048]{1,0:T(4,128)(2,1)S(1)}, u32[]{:S(2)}, u32[]{:S(2)}) collective-permute-start(bf16[4,2048]{1,0:T(4,128)(2,1)S(1)} %get-tuple-element.9), channel_id=1, source_target_pairs={{0,1},{1,2},{2,3},{3,0},{4,5},{5,6},{6,7},{7,4},{8,9},{9,10},{10,1... | collective-permute-start | bytes 49160 | tf_op jit(solution)/shard_map/ppermute | solution.py:45
  4.5 3.7 %all-to-all-start = ((bf16[4,8,1024]{2,0,1:T(4,128)(2,1)}), bf16[4,8,1024]{2,0,1:T(4,128)(2,1)S(1)}, u32[]{:S(2)}, u32[]{:S(2)}) async-start(bf16[4,8,1024]{2,0,1:T(4,128)(2,1)} %bitcast.22), calls=%async_computation | async-start | bytes 131072 | tf_op jit(solution)/shard_map/all_to_all | solution.py:40
  8.2 0.0 collective-permute-done
  8.3 1.6 %collective-permute-start.1 = (bf16[4,2048]{1,0:T(4,128)(2,1)S(1)}, bf16[4,2048]{1,0:T(4,128)(2,1)S(1)}, u32[]{:S(2)}, u32[]{:S(2)}) collective-permute-start(bf16[4,2048]{1,0:T(4,128)(2,1)S(1)} %collective-permute-done), channel_id=1, source_target_pairs={{0,1},{1,2},{2,3},{3,0},{4,5},{5,6},{6,7},{7,4},{8,9},{9,10},{10,1... | collective-permute-start | bytes 49160 | tf_op jit(solution)/shard_map/ppermute | solution.py:45
  9.9 9.7 %all-gather = bf16[8,4,2048]{2,1,0:T(4,128)(2,1)S(1)} all-gather(bf16[1,4,2048]{2,1,0:T(4,128)(2,1)S(1)} %get-tuple-element.10), channel_id=1, replica_groups=mesh['dp'=8,'mp'=4] {'dp'}, dimensions={0}, use_global_device_ids=true | all-gather | bytes 147456 | tf_op jit(solution)/shard_map/all_gather | solution.py:51
  19.6 0.0 collective-permute-done.1
  19.6 1.6 %collective-permute-start.2 = (bf16[4,2048]{1,0:T(4,128)(2,1)S(1)}, bf16[4,2048]{1,0:T(4,128)(2,1)S(1)}, u32[]{:S(2)}, u32[]{:S(2)}) collective-permute-start(bf16[4,2048]{1,0:T(4,128)(2,1)S(1)} %collective-permute-done.1), channel_id=1, source_target_pairs={{0,1},{1,2},{2,3},{3,0},{4,5},{5,6},{6,7},{7,4},{8,9},{9,10},{10,1... | collective-permute-start | bytes 49160 | tf_op jit(solution)/shard_map/ppermute | solution.py:45
  21.2 9.1 %all-gather.1 = bf16[8,4,2048]{2,1,0:T(4,128)(2,1)S(1)} all-gather(bf16[1,4,2048]{2,1,0:T(4,128)(2,1)} %bitcast.23), channel_id=1, replica_groups=mesh['dp'=8,'mp'=4] {'dp'}, dimensions={0}, use_global_device_ids=true | all-gather | bytes 147456 | tf_op jit(solution)/shard_map/all_gather | solution.py:53
  30.4 0.0 collective-permute-done.2
  30.5 0.8 constant_dynamic-update-slice_fusion.4
  31.3 0.8 constant_dynamic-update-slice_fusion
  32.0 0.7 constant_dynamic-slice_fusion
  32.7 0.0 all-to-all-done
  32.7 3.4 %all-to-all-start.1 = ((bf16[4,8,1024]{2,0,1:T(4,128)(2,1)}), bf16[4,8,1024]{2,0,1:T(4,128)(2,1)S(1)}, u32[]{:S(2)}, u32[]{:S(2)}) async-start(bf16[4,8,1024]{2,0,1:T(4,128)(2,1)} %bitcast.4), calls=%async_computation.1 | async-start | bytes 131072 | tf_op jit(solution)/shard_map/all_to_all | solution.py:49
  36.1 1.3 fusion.5
  37.4 0.0 copy-start
  37.4 3.4 %copy-done = f32[1024,2048]{1,0:T(8,128)} copy-done((f32[1024,2048]{1,0:T(8,128)}, f32[1024,2048]{1,0:T(8,128)S(1)}, u32[]{:S(2)}) %copy-start) | copy-done | bytes 8388632
  40.8 7.6 %fusion.2 = (f32[]{:T(128)}, f32[2048,1024]{0,1:T(8,128)}) fusion(f32[1024,2048]{1,0:T(8,128)S(1)} %fusion.5, bf16[32,2048]{1,0:T(8,128)(2,1)S(1)} %reshape.17, bf16[32,1024]{1,0:T(8,128)(2,1)S(1)} %all_to_all.31), kind=kOutput, calls=%fused_computation.4 | convolution fusion | flops 146800640 | bytes 16973828 | tf_op jit(solution)/shard_map/dot_general | solution.py:19
  48.4 0.0 all-to-all-done.1
  48.4 1.3 fusion.6
  49.7 0.0 copy-start.1
  49.7 7.8 %multiply_reduce_fusion = (f32[]{:T(128)}, f32[1024,2048]{1,0:T(8,128)}) fusion(f32[1024,2048]{1,0:T(8,128)S(1)} %fusion.6, bf16[32,1024]{1,0:T(8,128)(2,1)S(1)} %all_to_all.35, bf16[32,2048]{1,0:T(8,128)(2,1)S(1)} %reshape.19), kind=kOutput, calls=%fused_computation.6 | convolution fusion | flops 146800640 | bytes 16973828 | tf_op jit(solution)/shard_map/dot_general | solution.py:19
  57.5 0.0 copy-done.1
  58.8 39.7 %psum.7 = f32[]{:T(128)} all-reduce(f32[]{:T(128)S(6)} %add.37), channel_id=1, replica_groups=mesh['dp'=8,'mp'=4] {'dp','mp'}, use_global_device_ids=true, to_apply=%region_2.3 | all-reduce | flops 1 | bytes 8 | tf_op jit(solution)/shard_map/psum | solution.py:57
  99.2 29.9 %fusion = (f32[1024,2048]{1,0:T(8,128)}, f32[1024,2048]{1,0:T(8,128)}, f32[1024,2048]{1,0:T(8,128)}, f32[1024,2048]{1,0:T(8,128)}) fusion(f32[2048,1024]{0,1:T(8,128)} %get-tuple-element.12, f32[1024,2048]{1,0:T(8,128)} %copy-done, f32[]{:T(128)S(6)} %sqrt.3, f32[1024,2048]{1,0:T(8,128)} %copy-done.1, f32[1024,2048]{1,0:T(8,128)} %get-tuple-element.14), kind=kLoop, calls=%fused_computation.2 | loop fusion | flops 20971520 | bytes 67108864 | tf_op jit(solution)/shard_map/mul | solution.py:59
  (10 shorter events, 0.2 us)
Async XLA Ops:
  1.4 6.8 %collective-permute-start = (bf16[4,2048]{1,0:T(4,128)(2,1)S(1)}, bf16[4,2048]{1,0:T(4,128)(2,1)S(1)}, u32[]{:S(2)}, u32[]{:S(2)}) collective-permute-start(bf16[4,2048]{1,0:T(4,128)(2,1)S(1)} %get-tuple-element.9), channel_id=1, source_target_pairs={{0,1},{1,2},{2,3},{3,0},{4,5},{5,6},{6,7},{7,4},{8,9},{9,10},{10,1... | collective-permute-start | bytes 49160 | tf_op jit(solution)/shard_map/ppermute | solution.py:45
  4.5 28.2 %all-to-all-start = ((bf16[4,8,1024]{2,0,1:T(4,128)(2,1)}), bf16[4,8,1024]{2,0,1:T(4,128)(2,1)S(1)}, u32[]{:S(2)}, u32[]{:S(2)}) async-start(bf16[4,8,1024]{2,0,1:T(4,128)(2,1)} %bitcast.22), calls=%async_computation | async-start | bytes 131072 | tf_op jit(solution)/shard_map/all_to_all | solution.py:40
  8.3 11.3 %collective-permute-start.1 = (bf16[4,2048]{1,0:T(4,128)(2,1)S(1)}, bf16[4,2048]{1,0:T(4,128)(2,1)S(1)}, u32[]{:S(2)}, u32[]{:S(2)}) collective-permute-start(bf16[4,2048]{1,0:T(4,128)(2,1)S(1)} %collective-permute-done), channel_id=1, source_target_pairs={{0,1},{1,2},{2,3},{3,0},{4,5},{5,6},{6,7},{7,4},{8,9},{9,10},{10,1... | collective-permute-start | bytes 49160 | tf_op jit(solution)/shard_map/ppermute | solution.py:45
  19.6 10.8 %collective-permute-start.2 = (bf16[4,2048]{1,0:T(4,128)(2,1)S(1)}, bf16[4,2048]{1,0:T(4,128)(2,1)S(1)}, u32[]{:S(2)}, u32[]{:S(2)}) collective-permute-start(bf16[4,2048]{1,0:T(4,128)(2,1)S(1)} %collective-permute-done.1), channel_id=1, source_target_pairs={{0,1},{1,2},{2,3},{3,0},{4,5},{5,6},{6,7},{7,4},{8,9},{9,10},{10,1... | collective-permute-start | bytes 49160 | tf_op jit(solution)/shard_map/ppermute | solution.py:45
  32.7 15.7 %all-to-all-start.1 = ((bf16[4,8,1024]{2,0,1:T(4,128)(2,1)}), bf16[4,8,1024]{2,0,1:T(4,128)(2,1)S(1)}, u32[]{:S(2)}, u32[]{:S(2)}) async-start(bf16[4,8,1024]{2,0,1:T(4,128)(2,1)} %bitcast.4), calls=%async_computation.1 | async-start | bytes 131072 | tf_op jit(solution)/shard_map/all_to_all | solution.py:49
  37.4 3.4 %copy-start = (f32[1024,2048]{1,0:T(8,128)}, f32[1024,2048]{1,0:T(8,128)S(1)}, u32[]{:S(2)}) copy-start(f32[1024,2048]{1,0:T(8,128)S(1)} %fusion.5) | copy-start | bytes 25165828
  49.7 7.8 %copy-start.1 = (f32[1024,2048]{1,0:T(8,128)}, f32[1024,2048]{1,0:T(8,128)S(1)}, u32[]{:S(2)}) copy-start(f32[1024,2048]{1,0:T(8,128)S(1)} %fusion.6) | copy-start | bytes 25165828
